TPU v7x, 512 devices: a whole 4x4x16 slice. The times are simulated.
512 devices in a mesh: trial: 4 (over y), time: 32 (over z, core), chan: 4 (over x).
Axes of the slice: x: 4, y: 4, z: 16, core: 2. Of those that a mesh axis runs over, the one named last changes fastest.
Arguments:
- fade_rate: float32 [4, 8192, 2560], P('trial', 'time', 'chan'), parts along dimension 0, may hold values from 0.2 to 2
- update_in: bfloat16 [4, 8192, 2560], P('trial', 'time', 'chan'), parts along dimension 0, may hold values from -6 to 6
- gate_in: bfloat16 [4, 8192, 2560], P('trial', 'time', 'chan'), parts along dimension 0, may hold values from -6 to 6
- norm_gain: float32 [10240], P(('trial', 'chan')), parts along dimension 0, may hold values from 0.25 to 1.75
Outputs:
- sequence_out: bfloat16 [4, 8192, 2560], P('trial', 'time', 'chan'), parts along dimension 0
There are 4 independent parts, one for each index of `trial`. A program takes and returns all parts, laid end to end along the dimension named above; each array names one. Nothing has to cross between parts.
All inputs are finite; a program needn't handle non-finite values.
Results may differ from a plain program's by a relative error of at most 0.001.
Values sent between devices are 32-bit elements; how exact they have to be, the bound alone decides.
No kernel may reach another device: no remote copies, remote signals or barrier semaphores. Data moves between devices by JAX's collectives and lax.ppermute only.
A program may use at most 64 MiB of HBM per device.

v0:
```python
import jax
import jax.numpy as jnp
from jax import lax
from jax.sharding import Mesh
from jax.sharding import PartitionSpec as P

TIME = ("time_0", "time_1")


def sent_to_all(value, axis):
    length = lax.axis_size(axis)
    return lax.all_to_all(
        jnp.broadcast_to(value[None], (length, *value.shape)), axis, 0, 0, tiled=True
    )


def gathered_once(value, axis):
    leaves = jax.tree.leaves(value)
    sequence = sorted(range(len(leaves)), key=lambda k: -leaves[k].size)
    width = (1, *leaves[sequence[0]].shape)[-1]
    lines = [
        jnp.pad(leaves[k].reshape(-1), (0, -leaves[k].size % width)).reshape(-1, width)
        for k in sequence
    ]
    both, at, found = (sent_to_all(jnp.concatenate(lines), axis), 0, {})
    for k, line in zip(sequence, lines):
        share = both[:, at : at + len(line)].reshape(len(both), -1)
        found[k] = share[:, : leaves[k].size].reshape(-1, *leaves[k].shape)
        at += len(line)
    numbers = iter(range(len(leaves)))
    return jax.tree.map(lambda _: found[next(numbers)], value)


def joined_by_halves(pieces, combine):
    while len(jax.tree.leaves(pieces)[0]) > 1:
        pieces = jax.vmap(combine)(
            *(jax.tree.map(lambda part: part[side::2], pieces) for side in (0, 1))
        )
    return jax.tree.map(lambda part: part[0], pieces)


def carried_in(value, axis, combine, identity):
    length, place = (lax.axis_size(axis), lax.axis_index(axis))
    passed = jnp.arange(length) < place

    def kept(part, zero, own):
        part = jnp.where(
            passed.reshape(-1, *(1 for _ in own.shape)), part, jnp.asarray(zero, own.dtype)
        )
        return part

    pieces = gathered_once(value, axis)
    return joined_by_halves(jax.tree.map(kept, pieces, identity, value), combine)


def nothing_yet(value, identity):
    return jax.tree.map(
        lambda part, zero: jnp.zeros_like(part) + jnp.asarray(zero, part.dtype), value, identity
    )


def all_in_one(value, axis):
    leaves = jax.tree.leaves(value)
    sequence = sorted(range(len(leaves)), key=lambda k: -leaves[k].size)
    width = (1, *leaves[sequence[0]].shape)[-1]
    lines = [
        jnp.pad(leaves[k].reshape(-1), (0, -leaves[k].size % width)).reshape(-1, width)
        for k in sequence
    ]
    both, at, found = (lax.all_gather(jnp.concatenate(lines), axis), 0, {})
    for k, line in zip(sequence, lines):
        share = both[:, at : at + len(line)].reshape(len(both), -1)
        found[k] = share[:, : leaves[k].size].reshape(-1, *leaves[k].shape)
        at += len(line)
    numbers = iter(range(len(leaves)))
    return jax.tree.map(lambda _: found[next(numbers)], value)


def entering(value, axes, combine, identity):
    before = start = nothing_yet(value, identity)
    running = value
    for axis in reversed(axes):
        length, place = (lax.axis_size(axis), lax.axis_index(axis))
        pieces = all_in_one(running, axis)
        inside, running = (start, start)
        for k in reversed(range(length)):
            passed = k > place
            running = combine(running, jax.tree.map(lambda part: part[k], pieces))
            inside = jax.tree.map(lambda new, old: jnp.where(passed, new, old), running, inside)
        before = combine(inside, before)
    return before


def over_copies(value, axis):
    everything = sent_to_all(value, axis)
    return jnp.sum(everything, axis=0)


def join_pair(earlier, later):
    return (earlier[0] * later[0], later[0] * earlier[1] + later[1])


def per_device(fade_rate, update_in, gate_in, norm_gain):
    total_length = fade_rate.shape[1] * lax.axis_size(TIME)
    keep = jnp.exp(-fade_rate / total_length)
    push = update_in.astype(jnp.float32) * total_length ** (-0.5)
    product, forward = lax.associative_scan(join_pair, (keep, push), axis=1)
    entering_forward = carried_in(
        (product[:, -1], forward[:, -1]),
        TIME,
        join_pair,
        (jnp.ones_like(keep[:, 0]), jnp.zeros_like(push[:, 0])),
    )
    forward = forward + product * entering_forward[1][:, None]
    product, backward = lax.associative_scan(join_pair, (keep, push), axis=1, reverse=True)
    entering_backward = entering(
        (product[:, 0], backward[:, 0]),
        TIME,
        join_pair,
        (jnp.ones_like(keep[:, 0]), jnp.zeros_like(push[:, 0])),
    )
    backward = backward + product * entering_backward[1][:, None]
    states = forward + backward
    gated = states * jax.nn.sigmoid(gate_in.astype(jnp.float32))
    power = over_copies(jnp.sum(gated * gated, axis=-1, keepdims=True), "chan") / (
        gated.shape[-1] * lax.axis_size("chan")
    )
    sequence_out = (gated * lax.rsqrt(power + 1e-06) * norm_gain).astype(jnp.bfloat16)
    return sequence_out


def solution(mesh):
    torus = Mesh(
        mesh.devices.reshape(mesh.shape["trial"], 16, 2, mesh.shape["chan"]),
        ("trial", "time_0", "time_1", "chan"),
    )
    in_specs = (
        P("trial", TIME, "chan"),
        P("trial", TIME, "chan"),
        P("trial", TIME, "chan"),
        P(("trial", "chan")),
    )
    out_specs = P("trial", TIME, "chan")
    return jax.shard_map(
        per_device, mesh=torus, in_specs=in_specs, out_specs=out_specs, check_vma=False
    )
```

profile of v0, /device:TPU:24, one launch (start us, length us, event | category | flops | bytes accessed | tf_op | source)
XLA Modules:
  0.0 98.7 jit_solution(5250836695869192862)
XLA Ops:
  0.0 1.2 %multiply_exponential_fusion = f32[1,256,640]{2,1,0:T(8,128)S(1)} fusion(f32[1,256,640]{2,1,0:T(8,128)} %param.4), kind=kLoop, calls=%fused_computation.3 | loop fusion | flops 327680 | bytes 1310720 | tf_op jit(solution)/shard_map/exp | solution.py:105
  1.2 0.3 slice.700
  1.6 0.3 slice.696
  1.9 0.4 slice.695
  2.3 0.6 copy-done.8
  2.9 0.4 slice.752
  3.3 0.3 slice.698
  3.7 0.3 slice.697
  4.0 0.1 fusion.26
  4.1 0.1 slice.706
  4.2 0.1 slice.702
  4.4 0.2 slice.701
  4.6 0.2 slice.750
  4.8 0.1 slice.704
  4.9 0.1 slice.703
  7.3 0.8 add.507
  8.1 0.8 add.516
  8.8 0.8 add_multiply_fusion.2
  9.7 0.1 pad.210
  9.8 0.9 copy-done.7
  10.7 0.1 pad.226
  10.8 1.3 %pad.227 = f32[1,256,640]{2,1,0:T(8,128)S(1)} pad(f32[1,128,640]{2,1,0:T(8,128)} %add.516, f32[]{:T(128)} %constant.6.clone.1), padding=0_0_0x1_0_1x0_0_0 | pad | bytes 983044 | tf_op jit(solution)/shard_map/pad | solution.py:107
  12.1 2.8 %pad.211 = f32[1,256,640]{2,1,0:T(8,128)} pad(f32[1,128,640]{2,1,0:T(8,128)} %add.507, f32[]{:T(128)} %constant.6.clone.1), padding=0_0_0x1_0_1x0_0_0 | pad | bytes 983044 | tf_op jit(solution)/shard_map/pad | solution.py:107
  15.0 0.7 add_bitcast_fusion.2
  15.7 0.7 broadcast_in_dim.32
  16.4 15.5 %all-to-all-start = ((f32[32,2,640]{2,1,0:T(2,128)}), f32[32,2,640]{2,1,0:T(2,128)S(1)}, u32[]{:S(2)}, u32[]{:S(2)}) async-start(f32[32,2,640]{2,1,0:T(2,128)} %broadcast_in_dim.32), calls=%async_computation | async-start | bytes 327680 | tf_op jit(solution)/shard_map/all_to_all | solution.py:12
  31.9 0.1 slice.798
  32.1 0.1 slice.794
  32.2 0.3 slice.792
  32.6 0.6 copy-done.9
  33.2 0.3 reverse.9
  33.6 0.4 slice.850
  34.0 0.3 slice.796
  34.3 1.4 %slice.795 = f32[1,128,640]{2,1,0:T(8,128)} slice(f32[1,256,640]{2,1,0:T(8,128)S(1)} %broadcast_multiply_fusion), slice={[0:1:1], [0:255:2], [0:640:1]} | slice | bytes 655360 | tf_op jit(solution)/shard_map/slice | solution.py:115
  35.8 1.0 %fusion.27 = (f32[1,128,640]{2,1,0:T(8,128)S(1)}, f32[1,128,640]{2,1,0:T(8,128)S(1)}) fusion(f32[1,128,640]{2,1,0:T(8,128)S(1)} %slice.798, f32[1,128,640]{2,1,0:T(8,128)S(1)} %slice.794, f32[1,128,640]{2,1,0:T(8,128)S(1)} %slice.796, f32[1,128,640]{2,1,0:T(8,128)} %slice.795), kind=kLoop, calls=%fused_computation.194 | loop fusion | flops 245760 | bytes 1966080 | tf_op jit(solution)/shard_map/mul | solution.py:100
  36.8 0.1 slice.804
  36.9 0.1 slice.800
  37.1 0.2 slice.799
  37.3 0.2 slice.848
  37.5 0.1 slice.802
  37.6 0.1 slice.801
  38.8 0.2 slice.793
  40.2 0.8 add.545
  41.0 0.8 add.554
  41.7 0.1 add_multiply_fusion
  41.9 0.1 pad.242
  42.0 0.1 pad.258
  42.1 0.9 copy-done.6
  43.0 0.1 pad.259
  43.1 1.1 %pad.243 = f32[1,256,640]{2,1,0:T(8,128)S(1)} pad(f32[1,128,640]{2,1,0:T(8,128)} %add.545, f32[]{:T(128)} %constant.6.clone.1), padding=0_0_0x1_0_1x0_0_0 | pad | bytes 983044 | tf_op jit(solution)/shard_map/pad | solution.py:115
  44.2 0.9 add.555
  45.3 1.0 copy-done.5
  46.2 3.3 %rev.12 = f32[1,256,640]{2,1,0:T(8,128)} reverse(f32[1,256,640]{2,1,0:T(8,128)S(1)} %copy-done.5), dimensions={1} | reverse | bytes 1310720 | tf_op jit(solution)/shard_map/rev | solution.py:115
  49.5 3.3 %rev.11 = f32[1,256,640]{2,1,0:T(8,128)} reverse(f32[1,256,640]{2,1,0:T(8,128)S(1)} %add.547), dimensions={1} | reverse | bytes 1310720 | tf_op jit(solution)/shard_map/rev | solution.py:115
  52.8 1.9 %all-gather.2 = f32[2,2,640]{2,1,0:T(2,128)S(1)} all-gather(f32[1,2,640]{2,1,0:T(2,128)S(1)} %maximum_bitcast_fusion), channel_id=2, replica_groups=mesh['trial'=4,'time_0'=16,'time_1'=2,'chan'=4] {'time_1'}, dimensions={0}, use_global_device_ids=true | all-gather | bytes 15360 | tf_op jit(solution)/shard_map/all_gather | solution.py:70
  54.8 29.9 %all-gather.3 = f32[16,2,640]{2,1,0:T(2,128)S(1)} all-gather(f32[1,2,640]{2,1,0:T(2,128)S(1)} %maximum_bitcast_fusion.1), channel_id=3, replica_groups=mesh['trial'=4,'time_0'=16,'time_1'=2,'chan'=4] {'time_0'}, dimensions={0}, use_global_device_ids=true | all-gather | bytes 87040 | tf_op jit(solution)/shard_map/all_gather | solution.py:70
  84.8 0.1 fusion.24
  84.9 0.2 broadcast_select_fusion.1
  85.1 0.1 slice_multiply_fusion
  85.3 0.7 copy-done.10
  86.0 1.7 %multiply_reduce_fusion = (f32[256]{0:T(256)S(1)}, f32[1,256,640]{2,1,0:T(8,128)S(1)}) fusion(bf16[1,256,640]{2,1,0:T(8,128)(2,1)S(1)} %copy-done.10, f32[1,256,640]{2,1,0:T(8,128)} %rev.11, f32[1,256,640]{2,1,0:T(8,128)} %rev.12, f32[640]{0:T(1024)S(1)} %fusion.24, f32[640]{0:T(1024)S(1)} %fusion.22, f32[1,256,640]{2,1,0:T(8,128)S(1)} %copy-done.1, ...), kind=kLoop, calls=%fused_computation.1 | loop fusion | flops 2293504 | bytes 4921344 | tf_op jit(solution)/shard_map/reduce_sum | solution.py:125
  87.8 9.4 %all_to_all.10 = f32[4,1,256,1]{2,3,1,0:T(1,128)S(1)} all-to-all(f32[4,1,256,1]{2,3,1,0:T(1,128)S(1)} %broadcast_in_dim.35), channel_id=1, replica_groups=mesh['trial'=4,'time_0'=16,'time_1'=2,'chan'=4] {'chan'}, dimensions={0} | all-to-all | bytes 8192 | tf_op jit(solution)/shard_map/all_to_all | solution.py:12
  97.2 0.7 copy-done.11
  97.8 0.9 multiply_convert_fusion
  (237 shorter events, 4.0 us)
Async XLA Ops:
  1.9 1.0 copy-start.8
  9.7 1.0 copy-start.7
  10.8 4.2 %copy-start = (f32[1,256,640]{2,1,0:T(8,128)}, f32[1,256,640]{2,1,0:T(8,128)S(1)}, u32[]{:S(2)}) copy-start(f32[1,256,640]{2,1,0:T(8,128)S(1)} %pad.226) | copy-start | bytes 1966084
  12.1 4.3 %copy-start.2 = (f32[1,256,640]{2,1,0:T(8,128)}, f32[1,256,640]{2,1,0:T(8,128)S(1)}, u32[]{:S(2)}) copy-start(f32[1,256,640]{2,1,0:T(8,128)S(1)} %pad.227) | copy-start | bytes 1966084
  16.4 68.4 %all-to-all-start = ((f32[32,2,640]{2,1,0:T(2,128)}), f32[32,2,640]{2,1,0:T(2,128)S(1)}, u32[]{:S(2)}, u32[]{:S(2)}) async-start(f32[32,2,640]{2,1,0:T(2,128)} %broadcast_in_dim.32), calls=%async_computation | async-start | bytes 327680 | tf_op jit(solution)/shard_map/all_to_all | solution.py:12
  32.2 1.0 copy-start.9
  42.0 1.0 copy-start.6
  45.1 1.1 %copy-start.5 = (f32[1,256,640]{2,1,0:T(8,128)S(1)}, f32[1,256,640]{2,1,0:T(8,128)}, u32[]{:S(2)}) copy-start(f32[1,256,640]{2,1,0:T(8,128)} %add.555) | copy-start | bytes 1966084
  49.5 35.8 %copy-start.3 = (f32[1,256,640]{2,1,0:T(8,128)S(1)}, f32[1,256,640]{2,1,0:T(8,128)}, u32[]{:S(2)}) copy-start(f32[1,256,640]{2,1,0:T(8,128)} %copy-done.2) | copy-start | bytes 1966084
  49.5 35.8 %copy-start.4 = (f32[1,256,640]{2,1,0:T(8,128)S(1)}, f32[1,256,640]{2,1,0:T(8,128)}, u32[]{:S(2)}) copy-start(f32[1,256,640]{2,1,0:T(8,128)} %pad.211) | copy-start | bytes 1966084
  52.8 32.5 %copy-start.1 = (f32[1,256,640]{2,1,0:T(8,128)S(1)}, f32[1,256,640]{2,1,0:T(8,128)}, u32[]{:S(2)}) copy-start(f32[1,256,640]{2,1,0:T(8,128)} %copy-done) | copy-start | bytes 1966084
  85.1 1.0 copy-start.10
  97.1 0.7 copy-start.11
where the time goes:
time: 99.4 us; the launch traced here: 98.7 us
  blocking collectives  41.3 us (42%)
  local copies, waits for them, and re-layouts  27.9 us (28%)
  starting transfers between devices  15.5 us (16%)
  other arithmetic  12.4 us (12%)
  between operations  1.62 us (2%)
    all_gather x2, blocking collectives, all_in_one(): both, at, found = (lax.all_gather(jnp.concatenate(lines), axis), 0, {})  31.9 us
    all_to_all x1, starting transfers between devices, sent_to_all(): lax.all_to_all(jnp.broadcast_to(value[None], (length, *value.shape)), axi...  15.5 us
    all_to_all x1, blocking collectives, sent_to_all(): lax.all_to_all(jnp.broadcast_to(value[None], (length, *value.shape)), axi...  9.39 us
    rev x2, local copies, waits for them, and re-layouts, per_device(): lax.associative_scan(join_pair, (keep, push), axis=1, reverse=True)  6.59 us
    unnamed x24, local copies, waits for them, and re-layouts  5.31 us
    pad x28, local copies, waits for them, and re-layouts, per_device(): product, forward = lax.associative_scan(join_pair, (keep, push), axis=1)  4.81 us
    slice x52, local copies, waits for them, and re-layouts, per_device(): lax.associative_scan(join_pair, (keep, push), axis=1, reverse=True)  4.57 us
    slice x52, local copies, waits for them, and re-layouts, per_device(): product, forward = lax.associative_scan(join_pair, (keep, push), axis=1)  3.71 us
  transfers between devices with their start and end apart: 1, of which 0 were waited for; matrix products, arithmetic and copies ran while one was open for 18% of the time, Pallas kernels for 0%

commit v1 on v0

v1 whole, which is shorter than its diff:
```python
import functools

import jax
import jax.numpy as jnp
from jax import lax
from jax.experimental import pallas as pl
from jax.experimental.pallas import tpu as pltpu
from jax.sharding import Mesh
from jax.sharding import PartitionSpec as P

CHUNKS = ((0, 256), (256, 384))
SHIFT = 8


def dot_split(left, right):
    high = right.astype(jnp.bfloat16)
    low = (right - high.astype(jnp.float32)).astype(jnp.bfloat16)
    return jnp.dot(left, high, preferred_element_type=jnp.float32) + jnp.dot(
        left, low, preferred_element_type=jnp.float32
    )


def triangle(size, upper):
    row = lax.broadcasted_iota(jnp.int32, (size, size), 0)
    col = lax.broadcasted_iota(jnp.int32, (size, size), 1)
    keep = (col >= row) if upper else (col <= row)
    return keep.astype(jnp.float32).astype(jnp.bfloat16)


def copies(sources, targets, sems):
    rows = []
    for k, (at, width) in enumerate(CHUNKS):
        rows.append(
            [
                pltpu.make_async_copy(
                    s.at[:, pl.ds(at, width)], t.at[:, pl.ds(at, width)], sems.at[k, n]
                )
                for n, (s, t) in enumerate(zip(sources, targets))
            ]
        )
    for row in rows:
        for copy in row:
            copy.start()
    return rows


def summary_kernel(total, fade_hbm, push_hbm, out, fade, push, sems):
    rows = copies((fade_hbm, push_hbm), (fade, push), sems)
    lower = triangle(fade.shape[0], False)
    for (at, width), row in zip(CHUNKS, rows):
        for copy in row:
            copy.wait()
        cols = pl.ds(at, width)
        rate = fade[:, cols] * (1.0 / total)
        value = push[:, cols].astype(jnp.float32)
        run = dot_split(lower, rate)
        all_of = jnp.sum(rate, axis=0, keepdims=True)
        product = jnp.exp(-all_of)
        scale = total ** (-0.5)
        out[0:1, cols] = product
        out[1:2, cols] = (
            product * scale * jnp.sum(jnp.exp(run) * value, axis=0, keepdims=True)
        )
        out[2:3, cols] = scale * jnp.sum(jnp.exp(rate - run) * value, axis=0, keepdims=True)


def chip_kernel(both, out):
    place = lax.axis_index("z")
    p0, f0, b0 = (both[0, k : k + 1, :] for k in range(3))
    p1, f1, b1 = (both[1, k : k + 1, :] for k in range(3))
    product = p0 * p1
    forward = f1 + p1 * f0
    backward = b0 + p0 * b1
    count = out.shape[0]
    for k in range(count):
        out[k, 0:1, :] = product
        out[k, 1:2, :] = jnp.where(place < (k + SHIFT) % count, forward, backward)


def local_kernel(
    total, fade_hbm, push_hbm, gate_hbm, after, own, first, second, fade, push, gate, sems
):
    del after
    rows = copies((fade_hbm, push_hbm, gate_hbm), (fade, push, gate), sems)
    lower = triangle(fade.shape[0], False)
    upper = triangle(fade.shape[0], True)
    for (at, width), row in zip(CHUNKS, rows):
        for copy in row:
            copy.wait()
        cols = pl.ds(at, width)
        rate = fade[:, cols] * (1.0 / total)
        value = push[:, cols].astype(jnp.float32) * total ** (-0.5)
        gated = 1.0 / (1.0 + jnp.exp(-gate[:, cols].astype(jnp.float32)))
        run = dot_split(lower, rate)
        down = jnp.exp(-run)
        up = jnp.exp(run - rate)
        ahead = dot_split(lower, jnp.exp(run) * value)
        behind = dot_split(upper, jnp.exp(rate - run) * value)
        first[:, cols] = down * gated
        second[:, cols] = up * gated
        own[:, cols] = (down * ahead + up * behind) * gated


def join_kernel(both, others, own, first, second, gated, power):
    place, core = lax.axis_index("z"), lax.axis_index("core")
    count = others.shape[0]
    ahead = jnp.zeros_like(both[0, 0:1, :])
    behind = jnp.zeros_like(ahead)
    for k in range(count):
        at = (k + count - SHIFT) % count
        ahead = jnp.where(k < place, others[at, 0:1, :] * ahead + others[at, 1:2, :], ahead)
        j = count - 1 - k
        at = (j + count - SHIFT) % count
        behind = jnp.where(j > place, others[at, 0:1, :] * behind + others[at, 1:2, :], behind)
    p0, f0 = both[0, 0:1, :], both[0, 1:2, :]
    p1, b1 = both[1, 0:1, :], both[1, 2:3, :]
    low = core == 0
    ahead = jnp.where(low, ahead, f0 + p0 * ahead)
    behind = jnp.where(low, p0 * (b1 + p1 * behind), p1 * behind)
    lane = lax.broadcasted_iota(jnp.int32, (8, 128), 1)
    sums = jnp.zeros((8, 128), jnp.float32)
    for i in range(own.shape[0] // 8):
        rows = slice(8 * i, 8 * i + 8)
        value = own[rows, :] + first[rows, :] * ahead + second[rows, :] * behind
        gated[rows, :] = value
        part = jnp.sum(value * value, axis=1, keepdims=True)
        sums = jnp.where(lane == i, part, sums)
    for k in range(power.shape[0]):
        power[k] = sums


def norm_kernel(channels, powers, gated, gain, out_hbm, out, sems):
    power = powers[0] + powers[1] + powers[2] + powers[3]
    root = lax.rsqrt(power * (1.0 / channels) + 1e-06)
    weight = gain[...]
    count, pieces = out.shape[0] // 16, []
    for i in range(count):
        rows = slice(16 * i, 16 * i + 16)
        r = jnp.concatenate([root[:, 2 * i : 2 * i + 1], root[:, 2 * i + 1 : 2 * i + 2]], axis=0)
        out[rows, :] = (gated[rows, :] * r * weight).astype(jnp.bfloat16)
        if (i + 1) % (count // 2) == 0:
            half = (i + 1) // (count // 2) - 1
            size = out.shape[0] // 2
            piece = pltpu.make_async_copy(
                out.at[pl.ds(half * size, size), :],
                out_hbm.at[pl.ds(half * size, size), :],
                sems.at[half],
            )
            piece.start()
            pieces.append(piece)
    for piece in pieces:
        piece.wait()


ANY = pl.BlockSpec(memory_space=pl.ANY)
VMEM = pl.BlockSpec(memory_space=pltpu.VMEM)


def shape_of(*shape, dtype=jnp.float32):
    return jax.ShapeDtypeStruct(shape, dtype)


def per_device(fade_rate, update_in, gate_in, norm_gain):
    fade_rate, update_in, gate_in = fade_rate[0], update_in[0], gate_in[0]
    length, width = fade_rate.shape
    chips, chans = lax.axis_size("z"), lax.axis_size("chan")
    total = float(length * chips * lax.axis_size("core"))
    params = pltpu.CompilerParams(vmem_limit_bytes=16 * 2**20)
    f32, bf16 = jnp.float32, jnp.bfloat16
    block = (length, width)
    summary = pl.pallas_call(
        functools.partial(summary_kernel, total),
        out_shape=shape_of(3, width),
        in_specs=[ANY, ANY],
        out_specs=VMEM,
        scratch_shapes=[
            pltpu.VMEM(block, f32),
            pltpu.VMEM(block, bf16),
            pltpu.SemaphoreType.DMA((len(CHUNKS), 2)),
        ],
        compiler_params=params,
        name="summary",
    )(fade_rate, update_in)
    both = lax.all_gather(summary, "core")
    sent = pl.pallas_call(
        chip_kernel,
        out_shape=shape_of(chips, 2, width),
        in_specs=[VMEM],
        out_specs=VMEM,
        compiler_params=params,
        name="chip",
    )(both)
    order = [[(k + SHIFT) % chips for k in range(chips)]]
    others = lax.all_to_all(sent, "z", 0, 0, axis_index_groups=order, tiled=True)
    own, first, second = pl.pallas_call(
        functools.partial(local_kernel, total),
        out_shape=[shape_of(*block)] * 3,
        in_specs=[ANY] * 4,
        out_specs=[VMEM] * 3,
        scratch_shapes=[
            pltpu.VMEM(block, f32),
            pltpu.VMEM(block, bf16),
            pltpu.VMEM(block, bf16),
            pltpu.SemaphoreType.DMA((len(CHUNKS), 3)),
        ],
        compiler_params=params,
        cost_estimate=pl.CostEstimate(
            flops=1_000_000_000, bytes_accessed=4_000_000, transcendentals=1_000_000
        ),
        name="local",
    )(fade_rate, update_in, gate_in, sent)
    gated, power = pl.pallas_call(
        join_kernel,
        out_shape=[shape_of(*block), shape_of(chans, 8, 128)],
        in_specs=[VMEM] * 5,
        out_specs=[VMEM] * 2,
        compiler_params=params,
        name="join",
    )(both, others, own, first, second)
    powers = lax.all_to_all(power, "chan", 0, 0, tiled=True)
    out = pl.pallas_call(
        functools.partial(norm_kernel, float(width * chans)),
        out_shape=shape_of(*block, dtype=bf16),
        in_specs=[VMEM] * 3,
        out_specs=ANY,
        scratch_shapes=[pltpu.VMEM(block, bf16), pltpu.SemaphoreType.DMA((2,))],
        compiler_params=params,
        name="norm",
    )(powers, gated, norm_gain.reshape(1, width))
    return out[None]


def solution(mesh):
    torus = Mesh(
        mesh.devices.reshape(mesh.shape["trial"], mesh.shape["time"] // 2, 2, mesh.shape["chan"]),
        ("trial", "z", "core", "chan"),
    )
    time = ("z", "core")
    spec = P("trial", time, "chan")
    return jax.shard_map(
        per_device,
        mesh=torus,
        in_specs=(spec, spec, spec, P(("trial", "chan"))),
        out_specs=spec,
        check_vma=False,
    )
```

time: 99.4 us -> 40.9 us (0.41)
  the two profiles are of different devices: /device:TPU:24 before, /device:TPU:8 now
where the time goes in v1:
time: 40.9 us; the launch traced here: 40.6 us
  starting transfers between devices  23.3 us (57%)
  waiting for transfers between devices  7.32 us (18%)
  Pallas kernels  5.05 us (12%)
  local copies, waits for them, and re-layouts  3.04 us (7%)
  blocking collectives  1.82 us (4%)
    all_to_all x1, starting transfers between devices, per_device(): lax.all_to_all(sent, 'z', 0, 0, axis_index_groups=order, tiled=True)  18.9 us
    all_to_all x1, waiting for transfers between devices, per_device(): powers = lax.all_to_all(power, 'chan', 0, 0, tiled=True)  5.35 us
    all_to_all x1, starting transfers between devices, per_device(): powers = lax.all_to_all(power, 'chan', 0, 0, tiled=True)  4.43 us
    unnamed x12, local copies, waits for them, and re-layouts  3.04 us
    all_to_all x1, waiting for transfers between devices, per_device(): lax.all_to_all(sent, 'z', 0, 0, axis_index_groups=order, tiled=True)  1.97 us
    all_gather x1, blocking collectives, per_device(): both = lax.all_gather(summary, 'core')  1.82 us
    pallas_call x1, Pallas kernels, per_device(): pl.pallas_call(functools.partial(local_kernel, total), out_shape=[shape_o...  1.77 us
    pallas_call x1, Pallas kernels, per_device(): pl.pallas_call(functools.partial(norm_kernel, float(width * chans)), out_...  0.91 us
  transfers between devices with their start and end apart: 2, of which 2 were waited for; matrix products, arithmetic and copies ran while one was open for 0% of the time, Pallas kernels for 4%

profile of v1, /device:TPU:8, one launch (start us, length us, event | category | flops | bytes accessed | tf_op | source)
XLA Modules:
  0.0 40.6 jit_solution(16601481008193818426)
XLA Ops:
  0.0 0.0 copy-start
  0.0 1.1 %copy-done = f32[1,256,640]{2,1,0:T(8,128)S(1)} copy-done((f32[1,256,640]{2,1,0:T(8,128)S(1)}, f32[1,256,640]{2,1,0:T(8,128)}, u32[]{:S(2)}) %copy-start) | copy-done | bytes 655384
  1.1 0.0 copy-start.2
  1.1 1.0 %copy-done.2 = bf16[1,256,640]{2,1,0:T(8,128)(2,1)S(1)} copy-done((bf16[1,256,640]{2,1,0:T(8,128)(2,1)S(1)}, bf16[1,256,640]{2,1,0:T(8,128)(2,1)}, u32[]{:S(2)}) %copy-start.2) | copy-done | bytes 327704
  2.1 0.0 copy-start.1
  2.1 0.0 copy-start.3
  2.1 0.9 %summary.1 = f32[3,640]{1,0:T(4,128)S(1)} custom-call(f32[256,640]{1,0:T(8,128)S(1)} %bitcast.5, bf16[256,640]{1,0:T(8,128)(2,1)S(1)} %bitcast.7), custom_call_target="tpu_custom_call" | custom-call | tf_op jit(solution)/shard_map/summary/pallas_call | solution.py:171
  2.9 1.8 %all-gather.1.both = f32[2,3,640]{2,1,0:T(4,128)S(1)} all-gather(f32[1,3,640]{2,1,0:T(4,128)S(1)} %bitcast.9), channel_id=2, replica_groups=mesh['trial'=4,'z'=16,'core'=2,'chan'=4] {'core'}, dimensions={0}, use_global_device_ids=true | all-gather | bytes 23040 | tf_op jit(solution)/shard_map/all_gather | solution.py:184
  4.7 0.7 %chip.1.after = f32[16,2,640]{2,1,0:T(2,128)} custom-call(f32[2,3,640]{2,1,0:T(4,128)S(1)} %all-gather.1.both), custom_call_target="tpu_custom_call" | custom-call | tf_op jit(solution)/shard_map/chip/pallas_call | solution.py:185
  5.4 18.9 %all-to-all-start = ((f32[16,2,640]{2,1,0:T(2,128)}), f32[16,2,640]{2,1,0:T(2,128)S(1)}, u32[]{:S(2)}, u32[]{:S(2)}) async-start(f32[16,2,640]{2,1,0:T(2,128)} %chip.1.after), calls=%async_computation | async-start | bytes 163840 | tf_op jit(solution)/shard_map/all_to_all | solution.py:194
  24.3 0.0 copy-done.1
  24.3 0.0 copy-done.3
  24.3 0.0 copy-start.4
  24.3 1.0 %copy-done.4 = bf16[1,256,640]{2,1,0:T(8,128)(2,1)S(1)} copy-done((bf16[1,256,640]{2,1,0:T(8,128)(2,1)S(1)}, bf16[1,256,640]{2,1,0:T(8,128)(2,1)}, u32[]{:S(2)}) %copy-start.4) | copy-done | bytes 327704
  25.3 1.8 %local.1 = (f32[256,640]{1,0:T(8,128)S(1)}, f32[256,640]{1,0:T(8,128)S(1)}, f32[256,640]{1,0:T(8,128)S(1)}) custom-call(f32[256,640]{1,0:T(8,128)S(1)} %bitcast.6, bf16[256,640]{1,0:T(8,128)(2,1)S(1)} %bitcast.8, bf16[256,640]{1,0:T(8,128)(2,1)S(1)} %bitcast.10, f32[16,2,640]{2,1,0:T(2,128)} %chip.1.after), custom_call_target="tpu_custom_call" | custom-call | flops 1000000000 | bytes 4000000 | tf_op jit(solution)/shard_map/local/pallas_call | solution.py:195
  27.0 2.0 %all-to-all-done.others = f32[16,2,640]{2,1,0:T(2,128)S(1)} async-done(((f32[16,2,640]{2,1,0:T(2,128)}), f32[16,2,640]{2,1,0:T(2,128)S(1)}, u32[]{:S(2)}, u32[]{:S(2)}) %all-to-all-start) | async-done | bytes 81952 | tf_op jit(solution)/shard_map/all_to_all | solution.py:194
  29.0 0.9 %join.1 = (f32[256,640]{1,0:T(8,128)S(1)}, f32[4,8,128]{2,1,0:T(8,128)}) custom-call(f32[2,3,640]{2,1,0:T(4,128)S(1)} %all-gather.1.both, f32[16,2,640]{2,1,0:T(2,128)S(1)} %all-to-all-done.others, f32[256,640]{1,0:T(8,128)S(1)} %get-tuple-element.10.own, f32[256,640]{1,0:T(8,128)S(1)} %get-tuple-element.11.first, f32[256,640]{1,0:T(8,128)S(1)} %get-tuple-element.12.second), custom_call_target="tpu_custom_call" | custom-call | tf_op jit(solution)/shard_map/join/pallas_call | solution.py:212
  29.9 0.0 copy-start.5
  29.9 4.4 %all-to-all-start.1 = ((f32[4,8,128]{2,1,0:T(8,128)}), f32[4,8,128]{2,1,0:T(8,128)S(1)}, u32[]{:S(2)}, u32[]{:S(2)}) async-start(f32[4,8,128]{2,1,0:T(8,128)} %get-tuple-element.13), calls=%async_computation.1 | async-start | bytes 32768 | tf_op jit(solution)/shard_map/all_to_all | solution.py:220
  34.3 0.0 copy-done.5
  34.3 5.4 %all-to-all-done.1.powers = f32[4,8,128]{2,1,0:T(8,128)S(1)} async-done(((f32[4,8,128]{2,1,0:T(8,128)}), f32[4,8,128]{2,1,0:T(8,128)S(1)}, u32[]{:S(2)}, u32[]{:S(2)}) %all-to-all-start.1) | async-done | bytes 16416 | tf_op jit(solution)/shard_map/all_to_all | solution.py:220
  39.7 0.9 %norm.1 = bf16[256,640]{1,0:T(8,128)(2,1)} custom-call(f32[4,8,128]{2,1,0:T(8,128)S(1)} %all-to-all-done.1.powers, f32[256,640]{1,0:T(8,128)S(1)} %get-tuple-element.14.gated, f32[1,640]{1,0:T(1,128)S(1)} %reshape.3.gain), custom_call_target="tpu_custom_call" | custom-call | tf_op jit(solution)/shard_map/norm/pallas_call | solution.py:221
  (1 shorter events, 0.0 us)
Async XLA Ops:
  0.0 1.1 %copy-start = (f32[1,256,640]{2,1,0:T(8,128)S(1)}, f32[1,256,640]{2,1,0:T(8,128)}, u32[]{:S(2)}) copy-start(f32[1,256,640]{2,1,0:T(8,128)} %param.4) | copy-start | bytes 1966084
  1.1 1.0 %copy-start.2 = (bf16[1,256,640]{2,1,0:T(8,128)(2,1)S(1)}, bf16[1,256,640]{2,1,0:T(8,128)(2,1)}, u32[]{:S(2)}) copy-start(bf16[1,256,640]{2,1,0:T(8,128)(2,1)} %param.5) | copy-start | bytes 983044
  2.1 22.2 %copy-start.1 = (f32[1,256,640]{2,1,0:T(8,128)S(1)}, f32[1,256,640]{2,1,0:T(8,128)}, u32[]{:S(2)}) copy-start(f32[1,256,640]{2,1,0:T(8,128)} %param.4) | copy-start | bytes 1966084
  2.1 22.2 %copy-start.3 = (bf16[1,256,640]{2,1,0:T(8,128)(2,1)S(1)}, bf16[1,256,640]{2,1,0:T(8,128)(2,1)}, u32[]{:S(2)}) copy-start(bf16[1,256,640]{2,1,0:T(8,128)(2,1)} %param.5) | copy-start | bytes 983044
  5.4 23.6 %all-to-all-start = ((f32[16,2,640]{2,1,0:T(2,128)}), f32[16,2,640]{2,1,0:T(2,128)S(1)}, u32[]{:S(2)}, u32[]{:S(2)}) async-start(f32[16,2,640]{2,1,0:T(2,128)} %chip.1.after), calls=%async_computation | async-start | bytes 163840 | tf_op jit(solution)/shard_map/all_to_all | solution.py:194
  24.3 1.0 %copy-start.4 = (bf16[1,256,640]{2,1,0:T(8,128)(2,1)S(1)}, bf16[1,256,640]{2,1,0:T(8,128)(2,1)}, u32[]{:S(2)}) copy-start(bf16[1,256,640]{2,1,0:T(8,128)(2,1)} %param.6) | copy-start | bytes 983044
  29.9 4.4 %copy-start.5 = (f32[640]{0:T(1024)S(1)}, f32[640]{0:T(1024)}, u32[]{:S(2)}) copy-start(f32[640]{0:T(1024)} %param.7) | copy-start | bytes 7684
  29.9 9.8 %all-to-all-start.1 = ((f32[4,8,128]{2,1,0:T(8,128)}), f32[4,8,128]{2,1,0:T(8,128)S(1)}, u32[]{:S(2)}, u32[]{:S(2)}) async-start(f32[4,8,128]{2,1,0:T(8,128)} %get-tuple-element.13), calls=%async_computation.1 | async-start | bytes 32768 | tf_op jit(solution)/shard_map/all_to_all | solution.py:220

commit v2 on v1

v2 whole, which is shorter than its diff:
```python
import functools

import jax
import jax.numpy as jnp
from jax import lax
from jax.experimental import pallas as pl
from jax.experimental.pallas import tpu as pltpu
from jax.sharding import Mesh
from jax.sharding import PartitionSpec as P

CHUNKS = ((0, 384), (384, 256))
ORDER = (11, 12, 13, 14, 15, 0, 1, 2, 3, 4, 5, 6, 7, 8, 9, 10)
PIECES = 4
CHAN_ORDER = (2, 1, 0, 3)
EARLY = 3


def dot_split(left, right):
    high = right.astype(jnp.bfloat16)
    low = (right - high.astype(jnp.float32)).astype(jnp.bfloat16)
    return jnp.dot(left, high, preferred_element_type=jnp.float32) + jnp.dot(
        left, low, preferred_element_type=jnp.float32
    )


def triangle(size, upper):
    row = lax.broadcasted_iota(jnp.int32, (size, size), 0)
    col = lax.broadcasted_iota(jnp.int32, (size, size), 1)
    keep = (col >= row) if upper else (col <= row)
    return keep.astype(jnp.float32).astype(jnp.bfloat16)


def copies(sources, targets, sems):
    rows = []
    for k, (at, width) in enumerate(CHUNKS):
        rows.append(
            [
                pltpu.make_async_copy(
                    s.at[:, pl.ds(at, width)], t.at[:, pl.ds(at, width)], sems.at[k, n]
                )
                for n, (s, t) in enumerate(zip(sources, targets))
            ]
        )
    for row in rows:
        for copy in row:
            copy.start()
    return rows


def summary_kernel(
    total, fade_hbm, push_hbm, gate_hbm, gain_hbm, out, fade, push, gate, gain, sems, late_sems
):
    rows = copies((fade_hbm, push_hbm), (fade, push), sems)
    late = [
        pltpu.make_async_copy(gate_hbm, gate, late_sems.at[0]),
        pltpu.make_async_copy(gain_hbm, gain, late_sems.at[1]),
    ]
    for copy in late:
        copy.start()
    lower = triangle(fade.shape[0], False)
    for (at, width), row in zip(CHUNKS, rows):
        for copy in row:
            copy.wait()
        cols = pl.ds(at, width)
        rate = fade[:, cols] * (1.0 / total)
        value = push[:, cols].astype(jnp.float32)
        run = dot_split(lower, rate)
        all_of = jnp.sum(rate, axis=0, keepdims=True)
        product = jnp.exp(-all_of)
        scale = total ** (-0.5)
        out[0:1, cols] = product
        out[1:2, cols] = (
            product * scale * jnp.sum(jnp.exp(run) * value, axis=0, keepdims=True)
        )
        out[2:3, cols] = scale * jnp.sum(jnp.exp(rate - run) * value, axis=0, keepdims=True)
    for copy in late:
        copy.wait()


def local_parts(total, lower, upper, fade, push, gate, cols):
    rate = fade[:, cols] * (1.0 / total)
    value = push[:, cols].astype(jnp.float32) * total ** (-0.5)
    run = dot_split(lower, rate)
    down = jnp.exp(-run)
    up = jnp.exp(run - rate)
    ahead = dot_split(lower, jnp.exp(run) * value)
    behind = dot_split(upper, jnp.exp(rate - run) * value)
    share = 1.0 / (1.0 + jnp.exp(-gate[:, cols].astype(jnp.float32)))
    return down, up, ahead, behind, share


def chip_kernel(total, both, fade, push, gate, out, own, first, second):
    place = lax.axis_index("z")
    p0, f0, b0 = (both[0, k : k + 1, :] for k in range(3))
    p1, f1, b1 = (both[1, k : k + 1, :] for k in range(3))
    product = p0 * p1
    forward = f1 + p1 * f0
    backward = b0 + p0 * b1
    count = out.shape[0]
    for k in range(count):
        out[k, 0:1, :] = product
        out[k, 1:2, :] = jnp.where(place < ORDER[k], forward, backward)

    @pl.when(place < EARLY)
    def _():
        lower, upper = triangle(fade.shape[0], False), triangle(fade.shape[0], True)
        for at, width in CHUNKS:
            cols = pl.ds(at, width)
            down, up, ahead, behind, share = local_parts(
                total, lower, upper, fade, push, gate, cols
            )
            first[:, cols] = down * share
            second[:, cols] = up * share
            own[:, cols] = (down * ahead + up * behind) * share


def join_kernel(
    total, both, others, fade, push, gate, own, first, second, gain, gated, power, ends, total_sum
):
    place, core = lax.axis_index("z"), lax.axis_index("core")
    count = others.shape[0]
    ahead = jnp.zeros_like(both[0, 0:1, :])
    behind = jnp.zeros_like(ahead)
    for k in range(count):
        at = ORDER.index(k)
        ahead = jnp.where(k < place, others[at, 0:1, :] * ahead + others[at, 1:2, :], ahead)
        j = count - 1 - k
        at = ORDER.index(j)
        behind = jnp.where(j > place, others[at, 0:1, :] * behind + others[at, 1:2, :], behind)
    p0, f0 = both[0, 0:1, :], both[0, 1:2, :]
    p1, b1 = both[1, 0:1, :], both[1, 2:3, :]
    low = core == 0
    ends[0:1, :] = jnp.where(low, ahead, f0 + p0 * ahead)
    ends[1:2, :] = jnp.where(low, p0 * (b1 + p1 * behind), p1 * behind)
    for k in range(gain.shape[0] // 128):
        cols = pl.ds(128 * k, 128)
        ends[2:3, cols] = gain[cols].reshape(1, 128)
    lane = lax.broadcasted_iota(jnp.int32, (8, 128), 1)
    length = own.shape[0]

    @pl.when(place < EARLY)
    def _():
        ahead, behind, weight = ends[0:1, :], ends[1:2, :], ends[2:3, :]
        sums = jnp.zeros((8, 128), jnp.float32)
        for i in range(length // 8):
            rows = slice(8 * i, 8 * i + 8)
            value = own[rows, :] + first[rows, :] * ahead + second[rows, :] * behind
            gated[rows, :] = value * weight
            part = jnp.sum(value * value, axis=1, keepdims=True)
            sums = jnp.where(lane == i, part, sums)
        total_sum[...] = sums

    @pl.when(place >= EARLY)
    def _():
        lower, upper = triangle(length, False), triangle(length, True)
        squares = jnp.zeros((length, 128), jnp.float32)
        for at, width in CHUNKS:
            cols = pl.ds(at, width)
            down, up, mine, rest, share = local_parts(
                total, lower, upper, fade, push, gate, cols
            )
            value = (down * (mine + ends[0:1, cols]) + up * (rest + ends[1:2, cols])) * share
            gated[:, cols] = value * ends[2:3, cols]
            value = value * value
            for k in range(width // 128):
                squares = squares + value[:, 128 * k : 128 * k + 128]
        sums = jnp.zeros((8, 128), jnp.float32)
        for i in range(length // 8):
            part = jnp.sum(squares[8 * i : 8 * i + 8, :], axis=1, keepdims=True)
            sums = jnp.where(lane == i, part, sums)
        total_sum[...] = sums

    for k in range(power.shape[0]):
        power[k] = total_sum[...]


def norm_kernel(channels, powers, gated, out_hbm, out, sems):
    power = powers[0] + powers[1] + powers[2] + powers[3]
    root = lax.rsqrt(power * (1.0 / channels) + 1e-06)
    count, pieces = out.shape[0] // 16, []
    for i in range(count):
        rows = slice(16 * i, 16 * i + 16)
        r = jnp.concatenate([root[:, 2 * i : 2 * i + 1], root[:, 2 * i + 1 : 2 * i + 2]], axis=0)
        out[rows, :] = (gated[rows, :] * r).astype(jnp.bfloat16)
        if (i + 1) % (count // PIECES) == 0:
            half = (i + 1) // (count // PIECES) - 1
            size = out.shape[0] // PIECES
            piece = pltpu.make_async_copy(
                out.at[pl.ds(half * size, size), :],
                out_hbm.at[pl.ds(half * size, size), :],
                sems.at[half],
            )
            piece.start()
            pieces.append(piece)
    for piece in pieces:
        piece.wait()


ANY = pl.BlockSpec(memory_space=pl.ANY)
HBM = pl.BlockSpec(memory_space=pltpu.HBM)
VMEM = pl.BlockSpec(memory_space=pltpu.VMEM)


def shape_of(*shape, dtype=jnp.float32):
    return jax.ShapeDtypeStruct(shape, dtype)


def in_hbm(value):
    return pltpu.with_memory_space_constraint(value, pltpu.HBM)


def per_device(fade_rate, update_in, gate_in, norm_gain):
    fade_rate, update_in, gate_in = fade_rate[0], update_in[0], gate_in[0]
    length, width = fade_rate.shape
    chips, chans = lax.axis_size("z"), lax.axis_size("chan")
    total = float(length * chips * lax.axis_size("core"))
    params = pltpu.CompilerParams(vmem_limit_bytes=16 * 2**20)
    f32, bf16 = jnp.float32, jnp.bfloat16
    block = (length, width)
    summary, fade, push, gate, gain = pl.pallas_call(
        functools.partial(summary_kernel, total),
        out_shape=[
            shape_of(3, width),
            shape_of(*block),
            shape_of(*block, dtype=bf16),
            shape_of(*block, dtype=bf16),
            shape_of(width),
        ],
        in_specs=[HBM] * 4,
        out_specs=[VMEM] * 5,
        scratch_shapes=[
            pltpu.SemaphoreType.DMA((len(CHUNKS), 2)),
            pltpu.SemaphoreType.DMA((2,)),
        ],
        compiler_params=params,
        name="summary",
    )(in_hbm(fade_rate), in_hbm(update_in), in_hbm(gate_in), in_hbm(norm_gain))
    both = lax.all_gather(summary, "core")
    sent, own, first, second = pl.pallas_call(
        functools.partial(chip_kernel, total),
        out_shape=[shape_of(chips, 2, width)] + [shape_of(*block)] * 3,
        in_specs=[VMEM] * 4,
        out_specs=[VMEM] * 4,
        compiler_params=params,
        name="chip",
    )(both, fade, push, gate)
    others = lax.all_to_all(sent, "z", 0, 0, axis_index_groups=[list(ORDER)], tiled=True)
    gated, power = pl.pallas_call(
        functools.partial(join_kernel, total),
        out_shape=[shape_of(*block), shape_of(chans, 8, 128)],
        in_specs=[VMEM] * 9,
        out_specs=[VMEM] * 2,
        scratch_shapes=[pltpu.VMEM((3, width), f32), pltpu.VMEM((8, 128), f32)],
        compiler_params=params,
        name="join",
    )(both, others, fade, push, gate, own, first, second, gain)
    powers = lax.all_to_all(
        power, "chan", 0, 0, axis_index_groups=[list(CHAN_ORDER)], tiled=True
    )
    out = pl.pallas_call(
        functools.partial(norm_kernel, float(width * chans)),
        out_shape=shape_of(*block, dtype=bf16),
        in_specs=[VMEM] * 2,
        out_specs=ANY,
        scratch_shapes=[pltpu.VMEM(block, bf16), pltpu.SemaphoreType.DMA((PIECES,))],
        compiler_params=params,
        name="norm",
    )(powers, gated)
    return out[None]


def solution(mesh):
    torus = Mesh(
        mesh.devices.reshape(mesh.shape["trial"], mesh.shape["time"] // 2, 2, mesh.shape["chan"]),
        ("trial", "z", "core", "chan"),
    )
    time = ("z", "core")
    spec = P("trial", time, "chan")
    return jax.shard_map(
        per_device,
        mesh=torus,
        in_specs=(spec, spec, spec, P(("trial", "chan"))),
        out_specs=spec,
        check_vma=False,
    )
```

time: 40.9 us -> 36.2 us (0.89)
  the two profiles are of different devices: /device:TPU:8 before, /device:TPU:24 now
where the time goes in v2:
time: 36.2 us; the launch traced here: 36 us
  blocking collectives  31.3 us (86%)
  Pallas kernels  4.66 us (13%)
    all_to_all x1, blocking collectives, per_device(): lax.all_to_all(sent, 'z', 0, 0, axis_index_groups=[list(ORDER)], tiled=True)  21.7 us
    all_to_all x1, blocking collectives, per_device(): lax.all_to_all(power, 'chan', 0, 0, axis_index_groups=[list(CHAN_ORDER)],...  7.72 us
    pallas_call x1, Pallas kernels, per_device(): pl.pallas_call(functools.partial(summary_kernel, total), out_shape=[shape...  1.83 us
    all_gather x1, blocking collectives, per_device(): both = lax.all_gather(summary, 'core')  1.82 us
    pallas_call x1, Pallas kernels, per_device(): pl.pallas_call(functools.partial(chip_kernel, total), out_shape=[shape_of...  1.59 us
    pallas_call x1, Pallas kernels, per_device(): pl.pallas_call(functools.partial(norm_kernel, float(width * chans)), out_...  0.91 us

profile of v2, /device:TPU:24, one launch (start us, length us, event | category | flops | bytes accessed | tf_op | source)
XLA Modules:
  0.0 36.0 jit_solution(9193859567606331606)
XLA Ops:
  0.0 1.8 %summary.1 = (f32[3,640]{1,0:T(4,128)S(1)}, f32[256,640]{1,0:T(8,128)S(1)}, bf16[256,640]{1,0:T(8,128)(2,1)S(1)}, bf16[256,640]{1,0:T(8,128)(2,1)S(1)}, f32[640]{0:T(1024)S(1)}) custom-call(f32[256,640]{1,0:T(8,128)} %bitcast.6, bf16[256,640]{1,0:T(8,128)(2,1)} %bitcast.7, bf16[256,640]{1,0:T(8,128)(2,1)} %bitcast.8, f32[640]{0:T(1024)} %gain_hbm.1), custom_call_target="tpu_custom_call" | custom-call | tf_op jit(solution)/shard_map/summary/pallas_call | solution.py:220
  1.8 1.8 %all-gather.1.both = f32[2,3,640]{2,1,0:T(4,128)S(1)} all-gather(f32[1,3,640]{2,1,0:T(4,128)S(1)} %bitcast.5), channel_id=2, replica_groups=mesh['trial'=4,'z'=16,'core'=2,'chan'=4] {'core'}, dimensions={0}, use_global_device_ids=true | all-gather | bytes 23040 | tf_op jit(solution)/shard_map/all_gather | solution.py:238
  3.7 1.6 %chip.1 = (f32[16,2,640]{2,1,0:T(2,128)S(1)}, f32[256,640]{1,0:T(8,128)S(1)}, f32[256,640]{1,0:T(8,128)S(1)}, f32[256,640]{1,0:T(8,128)S(1)}) custom-call(f32[2,3,640]{2,1,0:T(4,128)S(1)} %all-gather.1.both, f32[256,640]{1,0:T(8,128)S(1)} %get-tuple-element.17.fade, bf16[256,640]{1,0:T(8,128)(2,1)S(1)} %get-tuple-element.18.push, ...), custom_call_target="tpu_custom_call" | custom-call | tf_op jit(solution)/shard_map/chip/pallas_call | solution.py:239
  5.3 21.7 %all_to_all.10.others = f32[16,2,640]{2,1,0:T(2,128)S(1)} all-to-all(f32[16,2,640]{2,1,0:T(2,128)S(1)} %get-tuple-element.20), channel_id=1, replica_groups={{88,96,104,112,120,0,8,16,24,32,40,48,56,64,72,80},{89,97,105,113,121,1..., dimensions={0} | all-to-all | bytes 163840 | tf_op jit(solution)/shard_map/all_to_all | solution.py:247
  27.0 0.3 join.1
  27.3 7.7 %all_to_all.11.powers = f32[4,8,128]{2,1,0:T(8,128)S(1)} all-to-all(f32[4,8,128]{2,1,0:T(8,128)S(1)} %get-tuple-element.25), channel_id=1, replica_groups={{2,1,0,3},{6,5,4,7},{10,9,8,11},{14,13,12,15},{18,17,16,19},{22,21,20,2..., dimensions={0} | all-to-all | bytes 32768 | tf_op jit(solution)/shard_map/all_to_all | solution.py:257
  35.1 0.9 %norm.1 = bf16[256,640]{1,0:T(8,128)(2,1)} custom-call(f32[4,8,128]{2,1,0:T(8,128)S(1)} %all_to_all.11.powers, f32[256,640]{1,0:T(8,128)S(1)} %get-tuple-element.26.gated), custom_call_target="tpu_custom_call" | custom-call | tf_op jit(solution)/shard_map/norm/pallas_call | solution.py:260

commit v3 on v2

--- a/solution.py
+++ b/solution.py
@@ -13,6 +13,7 @@
 PIECES = 4
 CHAN_ORDER = (2, 1, 0, 3)
 EARLY = 3
+NEAR = (0, 1, 2)
 
 
 def dot_split(left, right):
@@ -244,7 +245,8 @@
         compiler_params=params,
         name="chip",
     )(both, fade, push, gate)
-    others = lax.all_to_all(sent, "z", 0, 0, axis_index_groups=[list(ORDER)], tiled=True)
+    groups = [[2 * z + (c if z in NEAR else 1 - c) for z in ORDER] for c in (0, 1)]
+    others = lax.all_to_all(sent, ("z", "core"), 0, 0, axis_index_groups=groups, tiled=True)
     gated, power = pl.pallas_call(
         functools.partial(join_kernel, total),
         out_shape=[shape_of(*block), shape_of(chans, 8, 128)],

time: 36.2 us -> 35.8 us (0.989)
  the two profiles are of different devices: /device:TPU:24 before, /device:TPU:1 now
where the time goes in v3:
time: 35.8 us; the launch traced here: 35.6 us
  blocking collectives  30.9 us (86%)
  Pallas kernels  4.66 us (13%)
    all_to_all x1, blocking collectives, per_device(): lax.all_to_all(sent, ('z', 'core'), 0, 0, axis_index_groups=groups, tiled...  16.4 us
    all_gather x1, blocking collectives, per_device(): both = lax.all_gather(summary, 'core')  8.31 us
    all_to_all x1, blocking collectives, per_device(): lax.all_to_all(power, 'chan', 0, 0, axis_index_groups=[list(CHAN_ORDER)],...  6.23 us
    pallas_call x1, Pallas kernels, per_device(): pl.pallas_call(functools.partial(summary_kernel, total), out_shape=[shape...  1.83 us
    pallas_call x1, Pallas kernels, per_device(): pl.pallas_call(functools.partial(chip_kernel, total), out_shape=[shape_of...  1.59 us
    pallas_call x1, Pallas kernels, per_device(): pl.pallas_call(functools.partial(norm_kernel, float(width * chans)), out_...  0.91 us

profile of v3, /device:TPU:1, one launch (start us, length us, event | category | flops | bytes accessed | tf_op | source)
XLA Modules:
  0.0 35.6 jit_solution(1050183747819616494)
XLA Ops:
  0.0 1.8 %summary.1 = (f32[3,640]{1,0:T(4,128)S(1)}, f32[256,640]{1,0:T(8,128)S(1)}, bf16[256,640]{1,0:T(8,128)(2,1)S(1)}, bf16[256,640]{1,0:T(8,128)(2,1)S(1)}, f32[640]{0:T(1024)S(1)}) custom-call(f32[256,640]{1,0:T(8,128)} %bitcast.6, bf16[256,640]{1,0:T(8,128)(2,1)} %bitcast.7, bf16[256,640]{1,0:T(8,128)(2,1)} %bitcast.8, f32[640]{0:T(1024)} %gain_hbm.1), custom_call_target="tpu_custom_call" | custom-call | tf_op jit(solution)/shard_map/summary/pallas_call | solution.py:221
  1.8 8.3 %all-gather.1.both = f32[2,3,640]{2,1,0:T(4,128)S(1)} all-gather(f32[1,3,640]{2,1,0:T(4,128)S(1)} %bitcast.5), channel_id=2, replica_groups=mesh['trial'=4,'z'=16,'core'=2,'chan'=4] {'core'}, dimensions={0}, use_global_device_ids=true | all-gather | bytes 23040 | tf_op jit(solution)/shard_map/all_gather | solution.py:239
  10.2 1.6 %chip.1 = (f32[16,2,640]{2,1,0:T(2,128)S(1)}, f32[256,640]{1,0:T(8,128)S(1)}, f32[256,640]{1,0:T(8,128)S(1)}, f32[256,640]{1,0:T(8,128)S(1)}) custom-call(f32[2,3,640]{2,1,0:T(4,128)S(1)} %all-gather.1.both, f32[256,640]{1,0:T(8,128)S(1)} %get-tuple-element.17.fade, bf16[256,640]{1,0:T(8,128)(2,1)S(1)} %get-tuple-element.18.push, ...), custom_call_target="tpu_custom_call" | custom-call | tf_op jit(solution)/shard_map/chip/pallas_call | solution.py:240
  11.8 16.4 %all_to_all.10.others = f32[16,2,640]{2,1,0:T(2,128)S(1)} all-to-all(f32[16,2,640]{2,1,0:T(2,128)S(1)} %get-tuple-element.20), channel_id=1, replica_groups={{92,100,108,116,124,0,8,16,28,36,44,52,60,68,76,84},{88,96,104,112,120,..., dimensions={0} | all-to-all | bytes 163840 | tf_op jit(solution)/shard_map/all_to_all | solution.py:249
  28.1 0.3 join.1
  28.5 6.2 %all_to_all.11.powers = f32[4,8,128]{2,1,0:T(8,128)S(1)} all-to-all(f32[4,8,128]{2,1,0:T(8,128)S(1)} %get-tuple-element.25), channel_id=1, replica_groups={{2,1,0,3},{6,5,4,7},{10,9,8,11},{14,13,12,15},{18,17,16,19},{22,21,20,2..., dimensions={0} | all-to-all | bytes 32768 | tf_op jit(solution)/shard_map/all_to_all | solution.py:259
  34.7 0.9 %norm.1 = bf16[256,640]{1,0:T(8,128)(2,1)} custom-call(f32[4,8,128]{2,1,0:T(8,128)S(1)} %all_to_all.11.powers, f32[256,640]{1,0:T(8,128)S(1)} %get-tuple-element.26.gated), custom_call_target="tpu_custom_call" | custom-call | tf_op jit(solution)/shard_map/norm/pallas_call | solution.py:262

commit v4 on v3

--- a/solution.py
+++ b/solution.py
@@ -13,7 +13,7 @@
 PIECES = 4
 CHAN_ORDER = (2, 1, 0, 3)
 EARLY = 3
-NEAR = (0, 1, 2)
+NEAR = (0, 1)
 
 
 def dot_split(left, right):

time: 35.8 us -> 35.8 us (level)
  no operation moved by 1% of the time
where the time goes in v4:
time: 35.8 us; the launch traced here: 35.6 us
  blocking collectives  30.9 us (86%)
  Pallas kernels  4.66 us (13%)
    all_to_all x1, blocking collectives, per_device(): lax.all_to_all(sent, ('z', 'core'), 0, 0, axis_index_groups=groups, tiled...  16.4 us
    all_gather x1, blocking collectives, per_device(): both = lax.all_gather(summary, 'core')  8.31 us
    all_to_all x1, blocking collectives, per_device(): lax.all_to_all(power, 'chan', 0, 0, axis_index_groups=[list(CHAN_ORDER)],...  6.23 us
    pallas_call x1, Pallas kernels, per_device(): pl.pallas_call(functools.partial(summary_kernel, total), out_shape=[shape...  1.83 us
    pallas_call x1, Pallas kernels, per_device(): pl.pallas_call(functools.partial(chip_kernel, total), out_shape=[shape_of...  1.59 us
    pallas_call x1, Pallas kernels, per_device(): pl.pallas_call(functools.partial(norm_kernel, float(width * chans)), out_...  0.91 us

profile of v4, /device:TPU:1, one launch (start us, length us, event | category | flops | bytes accessed | tf_op | source)
XLA Modules:
  0.0 35.6 jit_solution(670240786510065462)
XLA Ops:
  0.0 1.8 %summary.1 = (f32[3,640]{1,0:T(4,128)S(1)}, f32[256,640]{1,0:T(8,128)S(1)}, bf16[256,640]{1,0:T(8,128)(2,1)S(1)}, bf16[256,640]{1,0:T(8,128)(2,1)S(1)}, f32[640]{0:T(1024)S(1)}) custom-call(f32[256,640]{1,0:T(8,128)} %bitcast.6, bf16[256,640]{1,0:T(8,128)(2,1)} %bitcast.7, bf16[256,640]{1,0:T(8,128)(2,1)} %bitcast.8, f32[640]{0:T(1024)} %gain_hbm.1), custom_call_target="tpu_custom_call" | custom-call | tf_op jit(solution)/shard_map/summary/pallas_call | solution.py:221
  1.8 8.3 %all-gather.1.both = f32[2,3,640]{2,1,0:T(4,128)S(1)} all-gather(f32[1,3,640]{2,1,0:T(4,128)S(1)} %bitcast.5), channel_id=2, replica_groups=mesh['trial'=4,'z'=16,'core'=2,'chan'=4] {'core'}, dimensions={0}, use_global_device_ids=true | all-gather | bytes 23040 | tf_op jit(solution)/shard_map/all_gather | solution.py:239
  10.2 1.6 %chip.1 = (f32[16,2,640]{2,1,0:T(2,128)S(1)}, f32[256,640]{1,0:T(8,128)S(1)}, f32[256,640]{1,0:T(8,128)S(1)}, f32[256,640]{1,0:T(8,128)S(1)}) custom-call(f32[2,3,640]{2,1,0:T(4,128)S(1)} %all-gather.1.both, f32[256,640]{1,0:T(8,128)S(1)} %get-tuple-element.17.fade, bf16[256,640]{1,0:T(8,128)(2,1)S(1)} %get-tuple-element.18.push, ...), custom_call_target="tpu_custom_call" | custom-call | tf_op jit(solution)/shard_map/chip/pallas_call | solution.py:240
  11.8 16.4 %all_to_all.10.others = f32[16,2,640]{2,1,0:T(2,128)S(1)} all-to-all(f32[16,2,640]{2,1,0:T(2,128)S(1)} %get-tuple-element.20), channel_id=1, replica_groups={{92,100,108,116,124,0,8,20,28,36,44,52,60,68,76,84},{88,96,104,112,120,..., dimensions={0} | all-to-all | bytes 163840 | tf_op jit(solution)/shard_map/all_to_all | solution.py:249
  28.1 0.3 join.1
  28.5 6.2 %all_to_all.11.powers = f32[4,8,128]{2,1,0:T(8,128)S(1)} all-to-all(f32[4,8,128]{2,1,0:T(8,128)S(1)} %get-tuple-element.25), channel_id=1, replica_groups={{2,1,0,3},{6,5,4,7},{10,9,8,11},{14,13,12,15},{18,17,16,19},{22,21,20,2..., dimensions={0} | all-to-all | bytes 32768 | tf_op jit(solution)/shard_map/all_to_all | solution.py:259
  34.7 0.9 %norm.1 = bf16[256,640]{1,0:T(8,128)(2,1)} custom-call(f32[4,8,128]{2,1,0:T(8,128)S(1)} %all_to_all.11.powers, f32[256,640]{1,0:T(8,128)S(1)} %get-tuple-element.26.gated), custom_call_target="tpu_custom_call" | custom-call | tf_op jit(solution)/shard_map/norm/pallas_call | solution.py:262

commit v5 on v3

--- a/solution.py
+++ b/solution.py
@@ -123,11 +123,12 @@
     ahead = jnp.zeros_like(both[0, 0:1, :])
     behind = jnp.zeros_like(ahead)
     for k in range(count):
-        at = ORDER.index(k)
-        ahead = jnp.where(k < place, others[at, 0:1, :] * ahead + others[at, 1:2, :], ahead)
         j = count - 1 - k
-        at = ORDER.index(j)
-        behind = jnp.where(j > place, others[at, 0:1, :] * behind + others[at, 1:2, :], behind)
+        at, back = ORDER.index(k), ORDER.index(j)
+        decay = jnp.where(k < place, others[at, 0:1, :], 1.0)
+        ahead = decay * ahead + jnp.where(k < place, others[at, 1:2, :], 0.0)
+        decay = jnp.where(j > place, others[back, 0:1, :], 1.0)
+        behind = decay * behind + jnp.where(j > place, others[back, 1:2, :], 0.0)
     p0, f0 = both[0, 0:1, :], both[0, 1:2, :]
     p1, b1 = both[1, 0:1, :], both[1, 2:3, :]
     low = core == 0

time: 35.8 us -> 35.8 us (level)
  no operation moved by 1% of the time
where the time goes in v5:
time: 35.8 us; the launch traced here: 35.6 us
  blocking collectives  30.9 us (86%)
  Pallas kernels  4.65 us (13%)
    all_to_all x1, blocking collectives, per_device(): lax.all_to_all(sent, ('z', 'core'), 0, 0, axis_index_groups=groups, tiled...  16.4 us
    all_gather x1, blocking collectives, per_device(): both = lax.all_gather(summary, 'core')  8.31 us
    all_to_all x1, blocking collectives, per_device(): lax.all_to_all(power, 'chan', 0, 0, axis_index_groups=[list(CHAN_ORDER)],...  6.23 us
    pallas_call x1, Pallas kernels, per_device(): pl.pallas_call(functools.partial(summary_kernel, total), out_shape=[shape...  1.83 us
    pallas_call x1, Pallas kernels, per_device(): pl.pallas_call(functools.partial(chip_kernel, total), out_shape=[shape_of...  1.59 us
    pallas_call x1, Pallas kernels, per_device(): pl.pallas_call(functools.partial(norm_kernel, float(width * chans)), out_...  0.91 us

profile of v5, /device:TPU:1, one launch (start us, length us, event | category | flops | bytes accessed | tf_op | source)
XLA Modules:
  0.0 35.6 jit_solution(18135137431778540438)
XLA Ops:
  0.0 1.8 %summary.1 = (f32[3,640]{1,0:T(4,128)S(1)}, f32[256,640]{1,0:T(8,128)S(1)}, bf16[256,640]{1,0:T(8,128)(2,1)S(1)}, bf16[256,640]{1,0:T(8,128)(2,1)S(1)}, f32[640]{0:T(1024)S(1)}) custom-call(f32[256,640]{1,0:T(8,128)} %bitcast.6, bf16[256,640]{1,0:T(8,128)(2,1)} %bitcast.7, bf16[256,640]{1,0:T(8,128)(2,1)} %bitcast.8, f32[640]{0:T(1024)} %gain_hbm.1), custom_call_target="tpu_custom_call" | custom-call | tf_op jit(solution)/shard_map/summary/pallas_call | solution.py:222
  1.8 8.3 %all-gather.1.both = f32[2,3,640]{2,1,0:T(4,128)S(1)} all-gather(f32[1,3,640]{2,1,0:T(4,128)S(1)} %bitcast.5), channel_id=2, replica_groups=mesh['trial'=4,'z'=16,'core'=2,'chan'=4] {'core'}, dimensions={0}, use_global_device_ids=true | all-gather | bytes 23040 | tf_op jit(solution)/shard_map/all_gather | solution.py:240
  10.2 1.6 %chip.1 = (f32[16,2,640]{2,1,0:T(2,128)S(1)}, f32[256,640]{1,0:T(8,128)S(1)}, f32[256,640]{1,0:T(8,128)S(1)}, f32[256,640]{1,0:T(8,128)S(1)}) custom-call(f32[2,3,640]{2,1,0:T(4,128)S(1)} %all-gather.1.both, f32[256,640]{1,0:T(8,128)S(1)} %get-tuple-element.17.fade, bf16[256,640]{1,0:T(8,128)(2,1)S(1)} %get-tuple-element.18.push, ...), custom_call_target="tpu_custom_call" | custom-call | tf_op jit(solution)/shard_map/chip/pallas_call | solution.py:241
  11.8 16.4 %all_to_all.10.others = f32[16,2,640]{2,1,0:T(2,128)S(1)} all-to-all(f32[16,2,640]{2,1,0:T(2,128)S(1)} %get-tuple-element.20), channel_id=1, replica_groups={{92,100,108,116,124,0,8,16,28,36,44,52,60,68,76,84},{88,96,104,112,120,..., dimensions={0} | all-to-all | bytes 163840 | tf_op jit(solution)/shard_map/all_to_all | solution.py:250
  28.1 0.3 join.1
  28.5 6.2 %all_to_all.11.powers = f32[4,8,128]{2,1,0:T(8,128)S(1)} all-to-all(f32[4,8,128]{2,1,0:T(8,128)S(1)} %get-tuple-element.25), channel_id=1, replica_groups={{2,1,0,3},{6,5,4,7},{10,9,8,11},{14,13,12,15},{18,17,16,19},{22,21,20,2..., dimensions={0} | all-to-all | bytes 32768 | tf_op jit(solution)/shard_map/all_to_all | solution.py:260
  34.7 0.9 %norm.1 = bf16[256,640]{1,0:T(8,128)(2,1)} custom-call(f32[4,8,128]{2,1,0:T(8,128)S(1)} %all_to_all.11.powers, f32[256,640]{1,0:T(8,128)S(1)} %get-tuple-element.26.gated), custom_call_target="tpu_custom_call" | custom-call | tf_op jit(solution)/shard_map/norm/pallas_call | solution.py:263

commit v6 on v4

--- a/solution.py
+++ b/solution.py
@@ -13,7 +13,7 @@
 PIECES = 4
 CHAN_ORDER = (2, 1, 0, 3)
 EARLY = 3
-NEAR = (0, 1)
+NEAR = (0, 1, 2, 8)
 
 
 def dot_split(left, right):

time: 35.8 us -> 35.8 us (level)
  no operation moved by 1% of the time
where the time goes in v6:
time: 35.8 us; the launch traced here: 35.6 us
  blocking collectives  31 us (87%)
  Pallas kernels  4.66 us (13%)
    all_to_all x1, blocking collectives, per_device(): lax.all_to_all(sent, ('z', 'core'), 0, 0, axis_index_groups=groups, tiled...  16.4 us
    all_gather x1, blocking collectives, per_device(): both = lax.all_gather(summary, 'core')  8.31 us
    all_to_all x1, blocking collectives, per_device(): lax.all_to_all(power, 'chan', 0, 0, axis_index_groups=[list(CHAN_ORDER)],...  6.26 us
    pallas_call x1, Pallas kernels, per_device(): pl.pallas_call(functools.partial(summary_kernel, total), out_shape=[shape...  1.83 us
    pallas_call x1, Pallas kernels, per_device(): pl.pallas_call(functools.partial(chip_kernel, total), out_shape=[shape_of...  1.59 us
    pallas_call x1, Pallas kernels, per_device(): pl.pallas_call(functools.partial(norm_kernel, float(width * chans)), out_...  0.91 us

profile of v6, /device:TPU:1, one launch (start us, length us, event | category | flops | bytes accessed | tf_op | source)
XLA Modules:
  0.0 35.6 jit_solution(16930729238794238580)
XLA Ops:
  0.0 1.8 %summary.1 = (f32[3,640]{1,0:T(4,128)S(1)}, f32[256,640]{1,0:T(8,128)S(1)}, bf16[256,640]{1,0:T(8,128)(2,1)S(1)}, bf16[256,640]{1,0:T(8,128)(2,1)S(1)}, f32[640]{0:T(1024)S(1)}) custom-call(f32[256,640]{1,0:T(8,128)} %bitcast.6, bf16[256,640]{1,0:T(8,128)(2,1)} %bitcast.7, bf16[256,640]{1,0:T(8,128)(2,1)} %bitcast.8, f32[640]{0:T(1024)} %gain_hbm.1), custom_call_target="tpu_custom_call" | custom-call | tf_op jit(solution)/shard_map/summary/pallas_call | solution.py:221
  1.8 8.3 %all-gather.1.both = f32[2,3,640]{2,1,0:T(4,128)S(1)} all-gather(f32[1,3,640]{2,1,0:T(4,128)S(1)} %bitcast.5), channel_id=2, replica_groups=mesh['trial'=4,'z'=16,'core'=2,'chan'=4] {'core'}, dimensions={0}, use_global_device_ids=true | all-gather | bytes 23040 | tf_op jit(solution)/shard_map/all_gather | solution.py:239
  10.2 1.6 %chip.1 = (f32[16,2,640]{2,1,0:T(2,128)S(1)}, f32[256,640]{1,0:T(8,128)S(1)}, f32[256,640]{1,0:T(8,128)S(1)}, f32[256,640]{1,0:T(8,128)S(1)}) custom-call(f32[2,3,640]{2,1,0:T(4,128)S(1)} %all-gather.1.both, f32[256,640]{1,0:T(8,128)S(1)} %get-tuple-element.17.fade, bf16[256,640]{1,0:T(8,128)(2,1)S(1)} %get-tuple-element.18.push, ...), custom_call_target="tpu_custom_call" | custom-call | tf_op jit(solution)/shard_map/chip/pallas_call | solution.py:240
  11.8 16.4 %all_to_all.10.others = f32[16,2,640]{2,1,0:T(2,128)S(1)} all-to-all(f32[16,2,640]{2,1,0:T(2,128)S(1)} %get-tuple-element.20), channel_id=1, replica_groups={{92,100,108,116,124,0,8,16,28,36,44,52,60,64,76,84},{88,96,104,112,120,..., dimensions={0} | all-to-all | bytes 163840 | tf_op jit(solution)/shard_map/all_to_all | solution.py:249
  28.1 0.3 join.1
  28.5 6.3 %all_to_all.11.powers = f32[4,8,128]{2,1,0:T(8,128)S(1)} all-to-all(f32[4,8,128]{2,1,0:T(8,128)S(1)} %get-tuple-element.25), channel_id=1, replica_groups={{2,1,0,3},{6,5,4,7},{10,9,8,11},{14,13,12,15},{18,17,16,19},{22,21,20,2..., dimensions={0} | all-to-all | bytes 32768 | tf_op jit(solution)/shard_map/all_to_all | solution.py:259
  34.7 0.9 %norm.1 = bf16[256,640]{1,0:T(8,128)(2,1)} custom-call(f32[4,8,128]{2,1,0:T(8,128)S(1)} %all_to_all.11.powers, f32[256,640]{1,0:T(8,128)S(1)} %get-tuple-element.26.gated), custom_call_target="tpu_custom_call" | custom-call | tf_op jit(solution)/shard_map/norm/pallas_call | solution.py:262
